TPU v7x, 256 devices: a whole 4x4x8 slice. The times are simulated.
256 devices in a mesh: req: 8 (over x, core), seq: 32 (over y, z).
Axes of the slice: x: 4, y: 4, z: 8, core: 2. Of those that a mesh axis runs over, the one named last changes fastest.
Arguments:
- query_nope: bfloat16 [16, 2, 128, 128], P('req', None, 'seq'), may hold values from -12 to 12
- query_rope: bfloat16 [16, 2, 8192], P('req', None, 'seq'), may hold values from -32 to 32
- key_absorb: bfloat16 [128, 128, 512], P('seq'), may hold values from -0.5 to 0.5
- value_up_matrix: bfloat16 [128, 512, 128], P('seq'), may hold values from -0.5 to 0.5
- latent_cache: bfloat16 [16, 131072, 512], P('req', 'seq'), may hold values from -6 to 6
- rope_cache: bfloat16 [16, 64, 131072], P('req', None, 'seq'), may hold values from -4 to 4
- new_latent: bfloat16 [16, 2, 512], P('req'), may hold values from -12 to 12
- new_rope: bfloat16 [16, 2, 64], P('req'), may hold values from -10 to 10
- lengths: int32 [16], P('req'), may hold values from 1 to 131072
- positions: int32 [16, 2], P('req'), may hold values from 0 to 8191
Outputs:
- head_outputs: bfloat16 [16, 2, 128, 128], P('req', None, 'seq')
All inputs are finite; a program needn't handle non-finite values.
Results may differ from a plain program's by a relative error of at most 0.0087.
Values may be sent and summed in bfloat16 or wider, within the bound.
A program may use at most 64 MiB of HBM per device.

v0:
```python
import jax
import jax.numpy as jnp
from jax import lax
from jax.sharding import PartitionSpec as P

BLOCK = 512


NEG_FILL = -1e30


def laid_out(parts, dim):
    parts = jnp.moveaxis(parts, 0, dim)
    shape = parts.shape
    return parts.reshape(*shape[:dim], shape[dim] * shape[dim + 1], *shape[dim + 2 :])


def gather_together(arrays, axis, dims):
    flat = jnp.concatenate([a.reshape(-1) for a in arrays])
    lines, at, gathered = (lax.all_gather(flat, axis), 0, [])
    for a, dim in zip(arrays, dims):
        parts = lines[:, at : at + a.size].reshape(-1, *a.shape)
        gathered.append(laid_out(parts, dim))
        at += a.size
    return tuple(gathered)


def partner(value, axis, bit):
    mask = 2**bit
    pairs = [(source, source ^ mask) for source in range(lax.axis_size(axis))]
    return lax.ppermute(value, axis, pairs)


def rotate(vectors, where_at):
    half_width = vectors.shape[-1] // 2
    frequency = 10000.0 ** (-jnp.arange(half_width, dtype=jnp.float32) / half_width)
    angles = where_at.astype(jnp.float32)[..., None] * frequency
    leading = vectors[..., :half_width].astype(jnp.float32)
    trailing = vectors[..., half_width:].astype(jnp.float32)
    return jnp.concatenate(
        [
            leading * jnp.cos(angles) - trailing * jnp.sin(angles),
            leading * jnp.sin(angles) + trailing * jnp.cos(angles),
        ],
        axis=-1,
    )


def attend(queries, rotary, latent_rows, rope_keys, live_keys, block_count, softmax_scale):
    row_count = queries.shape[0]
    start_state = (
        jnp.zeros((row_count, queries.shape[1]), jnp.float32),
        jnp.full((row_count,), NEG_FILL, jnp.float32),
        jnp.zeros((row_count,), jnp.float32),
    )

    def step_forward(block_index, state_now):
        weighted, maxima, totals = state_now
        offset = block_index * BLOCK
        latent_block = lax.dynamic_slice_in_dim(latent_rows, offset, BLOCK, 0)
        rope_block = lax.dynamic_slice_in_dim(rope_keys, offset, BLOCK, 1)
        scores = jnp.einsum("qk,tk->qt", queries, latent_block, preferred_element_type=jnp.float32)
        scores = (
            scores + jnp.dot(rotary, rope_block, preferred_element_type=jnp.float32)
        ) * softmax_scale
        is_valid_entry = offset + jnp.arange(BLOCK) < live_keys
        scores = jnp.where(is_valid_entry[None, :], scores, NEG_FILL)
        highest = jnp.maximum(maxima, jnp.max(scores, axis=1))
        shrink = jnp.exp(maxima - highest)
        softmax_probs = jnp.where(is_valid_entry[None, :], jnp.exp(scores - highest[:, None]), 0.0)
        weighted = weighted * shrink[:, None] + jnp.dot(
            softmax_probs.astype(jnp.bfloat16), latent_block, preferred_element_type=jnp.float32
        )
        return (weighted, highest, totals * shrink + jnp.sum(softmax_probs, axis=1))

    return lax.fori_loop(0, block_count, step_forward, start_state)


def combine(left_state, right_state):
    left_sums, left_maxima, left_totals = left_state
    right_sums, right_maxima, right_totals = right_state
    highest = jnp.maximum(left_maxima, right_maxima)
    left_factor = jnp.exp(left_maxima - highest)
    right_factor = jnp.exp(right_maxima - highest)
    return (
        left_sums * left_factor[..., None] + right_sums * right_factor[..., None],
        highest,
        left_totals * left_factor + right_totals * right_factor,
    )


def on_device(
    query_nope,
    query_rope,
    key_absorb,
    value_up_matrix,
    latent_cache,
    rope_cache,
    new_latent,
    new_rope,
    lengths,
    positions,
):
    groups, step_count, local_heads, nope_width = query_nope.shape
    latent_width = key_absorb.shape[2]
    rope_width = new_rope.shape[2]
    shard_keys = latent_cache.shape[1]
    shards = lax.axis_size("seq")
    shard_index = lax.axis_index("seq")
    softmax_scale = (nope_width + rope_width) ** (-0.5)
    query_latent = jnp.einsum(
        "rshn,hnk->rshk", query_nope, key_absorb, preferred_element_type=jnp.float32
    ).astype(jnp.bfloat16)
    gathered_latent, gathered_rope = gather_together((query_latent, query_rope), "seq", (2, 2))
    all_heads = gathered_latent.shape[2]
    first_key = shard_index * shard_keys
    results = []
    for request in range(groups):
        live_keys = jnp.clip(lengths[request] - first_key, 0, shard_keys)
        block_count = (live_keys + BLOCK - 1) // BLOCK
        queries = gathered_latent[request].reshape(step_count * all_heads, latent_width)
        rotary = gathered_rope[request].reshape(step_count * all_heads, rope_width)
        results.append(
            attend(
                queries,
                rotary,
                latent_cache[request],
                rope_cache[request],
                live_keys,
                block_count,
                softmax_scale,
            )
        )
    weighted = jnp.stack([piece[0] for piece in results]).reshape(
        groups, step_count, all_heads, latent_width
    )
    maxima = jnp.stack([piece[1] for piece in results]).reshape(groups, step_count, all_heads)
    totals = jnp.stack([piece[2] for piece in results]).reshape(groups, step_count, all_heads)
    state_now = (weighted, maxima, totals)
    for bit_index in reversed(range(shards.bit_length() - 1)):
        half_heads = state_now[1].shape[2] // 2
        is_upper = shard_index >> bit_index & 1 == 1
        lower_part = tuple((member[:, :, :half_heads] for member in state_now))
        upper_part = tuple((member[:, :, half_heads:] for member in state_now))
        kept = tuple(
            (
                jnp.where(is_upper, upper_member, lower_member)
                for lower_member, upper_member in zip(lower_part, upper_part)
            )
        )
        sent = tuple(
            (
                jnp.where(is_upper, lower_member, upper_member)
                for lower_member, upper_member in zip(lower_part, upper_part)
            )
        )
        received = partner(sent, "seq", bit_index)
        state_now = combine(kept, received)
    weighted, maxima, totals = state_now
    local_rope = query_rope.reshape(groups, step_count, local_heads, rope_width)
    key_new = rotate(new_rope, positions).astype(jnp.bfloat16)
    new_scores = jnp.einsum(
        "rshk,rjk->rshj", query_latent, new_latent, preferred_element_type=jnp.float32
    )
    new_scores = (
        new_scores
        + jnp.einsum("rshd,rjd->rshj", local_rope, key_new, preferred_element_type=jnp.float32)
    ) * softmax_scale
    causal = jnp.arange(step_count)[None, :] <= jnp.arange(step_count)[:, None]
    new_scores = jnp.where(causal[None, :, None, :], new_scores, NEG_FILL)
    highest = jnp.maximum(maxima, jnp.max(new_scores, axis=-1))
    shrink = jnp.exp(maxima - highest)
    new_weights = jnp.where(causal[None, :, None, :], jnp.exp(new_scores - highest[..., None]), 0.0)
    weighted = weighted * shrink[..., None] + jnp.einsum(
        "rshj,rjk->rshk",
        new_weights.astype(jnp.bfloat16),
        new_latent,
        preferred_element_type=jnp.float32,
    )
    totals = totals * shrink + jnp.sum(new_weights, axis=-1)
    latent_result = (weighted / totals[..., None]).astype(jnp.bfloat16)
    return jnp.einsum(
        "ufia,iaj->ufij", latent_result, value_up_matrix, preferred_element_type=jnp.float32
    ).astype(jnp.bfloat16)


def solution(mesh):
    return jax.shard_map(
        on_device,
        mesh=mesh,
        in_specs=(
            P("req", None, "seq", None),
            P("req", None, "seq"),
            P("seq", None, None),
            P("seq", None, None),
            P("req", "seq", None),
            P("req", None, "seq"),
            P("req", None, None),
            P("req", None, None),
            P("req"),
            P("req", None),
        ),
        out_specs=P("req", None, "seq", None),
        check_vma=False,
    )
```

profile of v0, /device:TPU:6, one launch (start us, length us, event | category | flops | bytes accessed | tf_op | source)
XLA Modules:
  0.0 177.9 jit_solution(17018369727087107778)
XLA Ops:
  0.0 1.3 fusion.77
  2.0 0.9 fusion.32
  2.9 0.7 copy.190
  3.6 53.0 %all-gather = bf16[294912]{0:T(1024)(128)(2,1)S(1)} all-gather(bf16[9216]{0:T(1024)(128)(2,1)S(1)} %pad_maximum_fusion), channel_id=2, replica_groups=mesh['req'=8,'seq'=32] {'seq'}, dimensions={0}, use_global_device_ids=true | all-gather | bytes 608256 | tf_op jit(solution)/shard_map/all_gather | solution.py:20
  57.6 0.4 reshape.88
  58.6 5.9 %slice_bitcast_fusion = (bf16[4096,512]{1,0:T(8,128)(2,1)}, bf16[4096,512]{1,0:T(8,128)(2,1)}) fusion(bf16[2,4096,512]{2,1,0:T(8,128)(2,1)} %param.18), kind=kLoop, calls=%fused_computation.42 | loop fusion | bytes 16777216 | tf_op jit(solution)/shard_map/squeeze | solution.py:127
  64.7 27.7 %while.29 = (s32[]{:T(128)}, f32[256,512]{1,0:T(8,128)S(1)}, f32[256]{0:T(256)S(1)}, f32[256]{0:T(256)S(1)}, s32[]{:T(128)}, /*index=5*/s32[]{:T(128)}, bf16[409...) while((s32[]{:T(128)}, f32[256,512]{1,0:T(8,128)S(1)}, ...), condition=%wide.region_7.8_spmd, body=%wide.region_4.7_spmd.sunk | while | flops 286787072 | bytes 5130439 | solution.py:76
  64.7 1.4 fusion.114
  66.6 1.5 convolution_add_fusion.7
  68.1 1.4 fusion.114
  70.0 1.6 convolution_add_fusion.7
  71.6 1.4 fusion.114
  73.5 1.5 convolution_add_fusion.7
  75.1 1.4 fusion.114
  76.9 1.6 convolution_add_fusion.7
  78.5 1.4 fusion.114
  80.4 1.5 convolution_add_fusion.7
  82.0 1.4 fusion.114
  83.9 1.6 convolution_add_fusion.7
  85.5 1.4 fusion.114
  87.3 1.5 convolution_add_fusion.7
  88.9 1.4 fusion.114
  90.8 1.6 convolution_add_fusion.7
  92.8 27.7 %while.28 = (s32[]{:T(128)}, f32[256,512]{1,0:T(8,128)S(1)}, f32[256]{0:T(256)S(1)}, f32[256]{0:T(256)S(1)}, s32[]{:T(128)}, /*index=5*/s32[]{:T(128)}, bf16[409...) while((s32[]{:T(128)}, f32[256,512]{1,0:T(8,128)S(1)}, ...), condition=%wide.region_3.4_spmd, body=%wide.region_0.3_spmd.sunk | while | flops 286787072 | bytes 5130439 | solution.py:76
  92.9 1.4 fusion.106
  94.7 1.5 convolution_add_fusion.6
  96.3 1.4 fusion.106
  98.2 1.6 convolution_add_fusion.6
  99.8 1.4 fusion.106
  101.7 1.5 convolution_add_fusion.6
  103.2 1.4 fusion.106
  105.1 1.6 convolution_add_fusion.6
  106.7 1.4 fusion.106
  108.6 1.5 convolution_add_fusion.6
  110.2 1.4 fusion.106
  112.1 1.6 convolution_add_fusion.6
  113.6 1.4 fusion.106
  115.5 1.5 convolution_add_fusion.6
  117.1 1.4 fusion.106
  119.0 1.6 convolution_add_fusion.6
  120.8 3.5 %collective-permute-start.10 = (f32[2,2,64]{2,1,0:T(2,128)S(1)}, f32[2,2,64]{2,1,0:T(2,128)S(1)}, u32[]{:S(2)}, u32[]{:S(2)}) collective-permute-start(f32[2,2,64]{2,1,0:T(2,128)S(1)} %broadcast_select_fusion.17), channel_id=1, source_target_pairs={{0,16},{1,17},{2,18},{3,19},{4,20},{5,21},{6,22},{7,23},{8,24},{9,... | collective-permute-start | bytes 3080 | tf_op jit(solution)/shard_map/ppermute | solution.py:31
  124.3 0.4 copy_dynamic-update-slice_fusion.1
  124.7 0.4 copy_dynamic-update-slice_fusion
  126.7 2.0 %collective-permute-start.2 = (f32[2,2,32]{2,1,0:T(2,128)S(1)}, f32[2,2,32]{2,1,0:T(2,128)S(1)}, u32[]{:S(2)}, u32[]{:S(2)}) collective-permute-start(f32[2,2,32]{2,1,0:T(2,128)S(1)} %broadcast_select_fusion.15), channel_id=1, source_target_pairs={{0,8},{1,9},{2,10},{3,11},{4,12},{5,13},{6,14},{7,15},{8,0},{9,1},... | collective-permute-start | bytes 1544 | tf_op jit(solution)/shard_map/ppermute | solution.py:31
  129.0 3.3 %collective-permute-done.11 = f32[2,2,32]{2,1,0:T(2,128)S(1)} collective-permute-done((f32[2,2,32]{2,1,0:T(2,128)S(1)}, f32[2,2,32]{2,1,0:T(2,128)S(1)}, u32[]{:S(2)}, u32[]{:S(2)}) %collective-permute-start.11) | collective-permute-done | bytes 544 | tf_op jit(solution)/shard_map/ppermute | solution.py:31
  132.5 3.6 %collective-permute-start.12 = (f32[2,2,16]{2,1,0:T(2,128)S(1)}, f32[2,2,16]{2,1,0:T(2,128)S(1)}, u32[]{:S(2)}, u32[]{:S(2)}) collective-permute-start(f32[2,2,16]{2,1,0:T(2,128)S(1)} %broadcast_select_fusion.11), channel_id=1, source_target_pairs={{0,4},{1,5},{2,6},{3,7},{4,0},{5,1},{6,2},{7,3},{8,12},{9,13},{10,... | collective-permute-start | bytes 776 | tf_op jit(solution)/shard_map/ppermute | solution.py:31
  136.2 2.4 %collective-permute-start.4 = (f32[2,2,16]{2,1,0:T(2,128)S(1)}, f32[2,2,16]{2,1,0:T(2,128)S(1)}, u32[]{:S(2)}, u32[]{:S(2)}) collective-permute-start(f32[2,2,16]{2,1,0:T(2,128)S(1)} %broadcast_select_fusion.12), channel_id=1, source_target_pairs={{0,4},{1,5},{2,6},{3,7},{4,0},{5,1},{6,2},{7,3},{8,12},{9,13},{10,... | collective-permute-start | bytes 776 | tf_op jit(solution)/shard_map/ppermute | solution.py:31
  138.7 1.3 collective-permute-done.12
  140.0 3.7 %collective-permute-done.4 = f32[2,2,16]{2,1,0:T(2,128)S(1)} collective-permute-done((f32[2,2,16]{2,1,0:T(2,128)S(1)}, f32[2,2,16]{2,1,0:T(2,128)S(1)}, u32[]{:S(2)}, u32[]{:S(2)}) %collective-permute-start.4) | collective-permute-done | bytes 288 | tf_op jit(solution)/shard_map/ppermute | solution.py:31
  144.2 2.8 %collective-permute-start.6 = (f32[2,2,8]{2,1,0:T(2,128)S(1)}, f32[2,2,8]{2,1,0:T(2,128)S(1)}, u32[]{:S(2)}, u32[]{:S(2)}) collective-permute-start(f32[2,2,8]{2,1,0:T(2,128)S(1)} %broadcast_select_fusion.9), channel_id=1, source_target_pairs={{0,2},{1,3},{2,0},{3,1},{4,6},{5,7},{6,4},{7,5},{8,10},{9,11},{10,... | collective-permute-start | bytes 392 | tf_op jit(solution)/shard_map/ppermute | solution.py:31
  147.2 1.1 collective-permute-done.13
  148.3 0.6 collective-permute-done.6
  149.0 0.5 multiply_add_fusion.2
  149.6 2.6 %collective-permute-start.3 = (f32[2,2,32,512]{3,1,0,2:T(2,128)S(1)}, f32[2,2,32,512]{3,1,0,2:T(2,128)S(1)}, u32[]{:S(2)}, u32[]{:S(2)}) collective-permute-start(f32[2,2,32,512]{3,1,0,2:T(2,128)S(1)} %broadcast_select_fusion.1), channel_id=1, source_target_pairs={{0,8},{1,9},{2,10},{3,11},{4,12},{5,13},{6,14},{7,15},{8,0},{9,1},... | collective-permute-start | bytes 786440 | tf_op jit(solution)/shard_map/ppermute | solution.py:31
  152.3 2.2 %collective-permute-start.8 = (f32[2,2,4]{2,1,0:T(2,128)S(1)}, f32[2,2,4]{2,1,0:T(2,128)S(1)}, u32[]{:S(2)}, u32[]{:S(2)}) collective-permute-start(f32[2,2,4]{2,1,0:T(2,128)S(1)} %broadcast_select_fusion.6), channel_id=1, source_target_pairs={{0,1},{1,0},{2,3},{3,2},{4,5},{5,4},{6,7},{7,6},{8,9},{9,8},{10,11... | collective-permute-start | bytes 200 | tf_op jit(solution)/shard_map/ppermute | solution.py:31
  154.8 1.8 collective-permute-done.3
  156.9 3.8 %collective-permute-start.5 = (f32[2,2,16,512]{3,1,0,2:T(2,128)S(1)}, f32[2,2,16,512]{3,1,0,2:T(2,128)S(1)}, u32[]{:S(2)}, u32[]{:S(2)}) collective-permute-start(f32[2,2,16,512]{3,1,0,2:T(2,128)S(1)} %broadcast_select_fusion.2), channel_id=1, source_target_pairs={{0,4},{1,5},{2,6},{3,7},{4,0},{5,1},{6,2},{7,3},{8,12},{9,13},{10,... | collective-permute-start | bytes 393224 | tf_op jit(solution)/shard_map/ppermute | solution.py:31
  160.8 5.2 %collective-permute-done.5 = f32[2,2,16,512]{3,1,0,2:T(2,128)S(1)} collective-permute-done((f32[2,2,16,512]{3,1,0,2:T(2,128)S(1)}, f32[2,2,16,512]{3,1,0,2:T(2,128)S(1)}, u32[]{:S(2)}, u32[]{:S(2)}) %collective-permute-start.5) | collective-permute-done | bytes 131104 | tf_op jit(solution)/shard_map/ppermute | solution.py:31
  166.2 3.8 %collective-permute-start.7 = (f32[2,2,8,512]{3,1,0,2:T(2,128)S(1)}, f32[2,2,8,512]{3,1,0,2:T(2,128)S(1)}, u32[]{:S(2)}, u32[]{:S(2)}) collective-permute-start(f32[2,2,8,512]{3,1,0,2:T(2,128)S(1)} %broadcast_select_fusion.3), channel_id=1, source_target_pairs={{0,2},{1,3},{2,0},{3,1},{4,6},{5,7},{6,4},{7,5},{8,10},{9,11},{10,... | collective-permute-start | bytes 196616 | tf_op jit(solution)/shard_map/ppermute | solution.py:31
  170.0 2.2 %collective-permute-done.7 = f32[2,2,8,512]{3,1,0,2:T(2,128)S(1)} collective-permute-done((f32[2,2,8,512]{3,1,0,2:T(2,128)S(1)}, f32[2,2,8,512]{3,1,0,2:T(2,128)S(1)}, u32[]{:S(2)}, u32[]{:S(2)}) %collective-permute-start.7) | collective-permute-done | bytes 65568 | tf_op jit(solution)/shard_map/ppermute | solution.py:31
  172.3 2.8 %collective-permute-start.9 = (f32[2,2,4,512]{3,1,0,2:T(2,128)S(1)}, f32[2,2,4,512]{3,1,0,2:T(2,128)S(1)}, u32[]{:S(2)}, u32[]{:S(2)}) collective-permute-start(f32[2,2,4,512]{3,1,0,2:T(2,128)S(1)} %broadcast_select_fusion.4), channel_id=1, source_target_pairs={{0,1},{1,0},{2,3},{3,2},{4,5},{5,4},{6,7},{7,6},{8,9},{9,8},{10,11... | collective-permute-start | bytes 98312 | tf_op jit(solution)/shard_map/ppermute | solution.py:31
  175.7 1.3 collective-permute-done.9
  177.0 0.3 fusion.36
  177.3 0.6 copy.180
  (191 shorter events, 14.1 us)
Async XLA Ops:
  0.0 2.0 %copy-start = (bf16[4,128,512]{2,1,0:T(8,128)(2,1)S(1)}, bf16[4,128,512]{2,1,0:T(8,128)(2,1)}, u32[]{:S(2)}) copy-start(bf16[4,128,512]{2,1,0:T(8,128)(2,1)} %param.16) | copy-start | bytes 1572868
  58.6 5.9 %copy-start.1 = (bf16[2,64,4096]{2,1,0:T(8,128)(2,1)S(1)}, bf16[2,64,4096]{2,1,0:T(8,128)(2,1)}, u32[]{:S(2)}) copy-start(bf16[2,64,4096]{2,1,0:T(8,128)(2,1)} %param.19) | copy-start | bytes 3145732
  92.8 32.8 %copy-start.2 = (bf16[2,2,256]{2,1,0:T(2,128)(2,1)S(1)}, bf16[2,2,256]{2,1,0:T(2,128)(2,1)}, u32[]{:S(2)}) copy-start(bf16[2,2,256]{2,1,0:T(2,128)(2,1)} %param.15) | copy-start | bytes 6148
  92.8 32.9 %copy-start.6 = (bf16[2,2,512]{2,1,0:T(2,128)(2,1)S(1)}, bf16[2,2,512]{2,1,0:T(2,128)(2,1)}, u32[]{:S(2)}) copy-start(bf16[2,2,512]{2,1,0:T(2,128)(2,1)} %param.20) | copy-start | bytes 12292
  92.8 33.2 %copy-start.4 = (s32[2,2]{1,0:T(2,128)S(1)}, s32[2,2]{1,0:T(2,128)}, u32[]{:S(2)}) copy-start(s32[2,2]{1,0:T(2,128)} %param.23) | copy-start | bytes 52
  92.8 33.2 %copy-start.3 = (bf16[2,2,64]{2,1,0:T(2,128)(2,1)S(1)}, bf16[2,2,64]{2,1,0:T(2,128)(2,1)}, u32[]{:S(2)}) copy-start(bf16[2,2,64]{2,1,0:T(2,128)(2,1)} %param.21) | copy-start | bytes 1540
  120.6 5.8 %collective-permute-start = (f32[2,2,64]{2,1,0:T(2,128)S(1)}, f32[2,2,64]{2,1,0:T(2,128)S(1)}, u32[]{:S(2)}, u32[]{:S(2)}) collective-permute-start(f32[2,2,64]{2,1,0:T(2,128)S(1)} %broadcast_select_fusion.18), channel_id=1, source_target_pairs={{0,16},{1,17},{2,18},{3,19},{4,20},{5,21},{6,22},{7,23},{8,24},{9,... | collective-permute-start | bytes 3080 | tf_op jit(solution)/shard_map/ppermute | solution.py:31
  120.8 5.6 %collective-permute-start.10 = (f32[2,2,64]{2,1,0:T(2,128)S(1)}, f32[2,2,64]{2,1,0:T(2,128)S(1)}, u32[]{:S(2)}, u32[]{:S(2)}) collective-permute-start(f32[2,2,64]{2,1,0:T(2,128)S(1)} %broadcast_select_fusion.17), channel_id=1, source_target_pairs={{0,16},{1,17},{2,18},{3,19},{4,20},{5,21},{6,22},{7,23},{8,24},{9,... | collective-permute-start | bytes 3080 | tf_op jit(solution)/shard_map/ppermute | solution.py:31
  125.2 51.8 %copy-start.5 = (bf16[4,512,128]{2,1,0:T(8,128)(2,1)S(1)}, bf16[4,512,128]{2,1,0:T(8,128)(2,1)}, u32[]{:S(2)}) copy-start(bf16[4,512,128]{2,1,0:T(8,128)(2,1)} %param.17) | copy-start | bytes 1572868
  125.5 23.5 %collective-permute-start.1 = (f32[2,2,64,512]{3,1,0,2:T(2,128)S(1)}, f32[2,2,64,512]{3,1,0,2:T(2,128)S(1)}, u32[]{:S(2)}, u32[]{:S(2)}) collective-permute-start(f32[2,2,64,512]{3,1,0,2:T(2,128)S(1)} %broadcast_select_fusion), channel_id=1, source_target_pairs={{0,16},{1,17},{2,18},{3,19},{4,20},{5,21},{6,22},{7,23},{8,24},{9,... | collective-permute-start | bytes 1572872 | tf_op jit(solution)/shard_map/ppermute | solution.py:31
  126.6 5.7 %collective-permute-start.11 = (f32[2,2,32]{2,1,0:T(2,128)S(1)}, f32[2,2,32]{2,1,0:T(2,128)S(1)}, u32[]{:S(2)}, u32[]{:S(2)}) collective-permute-start(f32[2,2,32]{2,1,0:T(2,128)S(1)} %broadcast_select_fusion.14), channel_id=1, source_target_pairs={{0,8},{1,9},{2,10},{3,11},{4,12},{5,13},{6,14},{7,15},{8,0},{9,1},... | collective-permute-start | bytes 1544 | tf_op jit(solution)/shard_map/ppermute | solution.py:31
  126.7 5.6 %collective-permute-start.2 = (f32[2,2,32]{2,1,0:T(2,128)S(1)}, f32[2,2,32]{2,1,0:T(2,128)S(1)}, u32[]{:S(2)}, u32[]{:S(2)}) collective-permute-start(f32[2,2,32]{2,1,0:T(2,128)S(1)} %broadcast_select_fusion.15), channel_id=1, source_target_pairs={{0,8},{1,9},{2,10},{3,11},{4,12},{5,13},{6,14},{7,15},{8,0},{9,1},... | collective-permute-start | bytes 1544 | tf_op jit(solution)/shard_map/ppermute | solution.py:31
  132.5 7.5 %collective-permute-start.12 = (f32[2,2,16]{2,1,0:T(2,128)S(1)}, f32[2,2,16]{2,1,0:T(2,128)S(1)}, u32[]{:S(2)}, u32[]{:S(2)}) collective-permute-start(f32[2,2,16]{2,1,0:T(2,128)S(1)} %broadcast_select_fusion.11), channel_id=1, source_target_pairs={{0,4},{1,5},{2,6},{3,7},{4,0},{5,1},{6,2},{7,3},{8,12},{9,13},{10,... | collective-permute-start | bytes 776 | tf_op jit(solution)/shard_map/ppermute | solution.py:31
  136.2 7.5 %collective-permute-start.4 = (f32[2,2,16]{2,1,0:T(2,128)S(1)}, f32[2,2,16]{2,1,0:T(2,128)S(1)}, u32[]{:S(2)}, u32[]{:S(2)}) collective-permute-start(f32[2,2,16]{2,1,0:T(2,128)S(1)} %broadcast_select_fusion.12), channel_id=1, source_target_pairs={{0,4},{1,5},{2,6},{3,7},{4,0},{5,1},{6,2},{7,3},{8,12},{9,13},{10,... | collective-permute-start | bytes 776 | tf_op jit(solution)/shard_map/ppermute | solution.py:31
  143.8 4.5 %collective-permute-start.13 = (f32[2,2,8]{2,1,0:T(2,128)S(1)}, f32[2,2,8]{2,1,0:T(2,128)S(1)}, u32[]{:S(2)}, u32[]{:S(2)}) collective-permute-start(f32[2,2,8]{2,1,0:T(2,128)S(1)} %broadcast_select_fusion.8), channel_id=1, source_target_pairs={{0,2},{1,3},{2,0},{3,1},{4,6},{5,7},{6,4},{7,5},{8,10},{9,11},{10,... | collective-permute-start | bytes 392 | tf_op jit(solution)/shard_map/ppermute | solution.py:31
  144.2 4.7 %collective-permute-start.6 = (f32[2,2,8]{2,1,0:T(2,128)S(1)}, f32[2,2,8]{2,1,0:T(2,128)S(1)}, u32[]{:S(2)}, u32[]{:S(2)}) collective-permute-start(f32[2,2,8]{2,1,0:T(2,128)S(1)} %broadcast_select_fusion.9), channel_id=1, source_target_pairs={{0,2},{1,3},{2,0},{3,1},{4,6},{5,7},{6,4},{7,5},{8,10},{9,11},{10,... | collective-permute-start | bytes 392 | tf_op jit(solution)/shard_map/ppermute | solution.py:31
  149.6 6.9 %collective-permute-start.3 = (f32[2,2,32,512]{3,1,0,2:T(2,128)S(1)}, f32[2,2,32,512]{3,1,0,2:T(2,128)S(1)}, u32[]{:S(2)}, u32[]{:S(2)}) collective-permute-start(f32[2,2,32,512]{3,1,0,2:T(2,128)S(1)} %broadcast_select_fusion.1), channel_id=1, source_target_pairs={{0,8},{1,9},{2,10},{3,11},{4,12},{5,13},{6,14},{7,15},{8,0},{9,1},... | collective-permute-start | bytes 786440 | tf_op jit(solution)/shard_map/ppermute | solution.py:31
  152.3 8.4 %collective-permute-start.8 = (f32[2,2,4]{2,1,0:T(2,128)S(1)}, f32[2,2,4]{2,1,0:T(2,128)S(1)}, u32[]{:S(2)}, u32[]{:S(2)}) collective-permute-start(f32[2,2,4]{2,1,0:T(2,128)S(1)} %broadcast_select_fusion.6), channel_id=1, source_target_pairs={{0,1},{1,0},{2,3},{3,2},{4,5},{5,4},{6,7},{7,6},{8,9},{9,8},{10,11... | collective-permute-start | bytes 200 | tf_op jit(solution)/shard_map/ppermute | solution.py:31
  154.6 20.5 %collective-permute-start.14 = (f32[2,2,4]{2,1,0:T(2,128)S(1)}, f32[2,2,4]{2,1,0:T(2,128)S(1)}, u32[]{:S(2)}, u32[]{:S(2)}) collective-permute-start(f32[2,2,4]{2,1,0:T(2,128)S(1)} %broadcast_select_fusion.5), channel_id=1, source_target_pairs={{0,1},{1,0},{2,3},{3,2},{4,5},{5,4},{6,7},{7,6},{8,9},{9,8},{10,11... | collective-permute-start | bytes 200 | tf_op jit(solution)/shard_map/ppermute | solution.py:31
  156.9 9.1 %collective-permute-start.5 = (f32[2,2,16,512]{3,1,0,2:T(2,128)S(1)}, f32[2,2,16,512]{3,1,0,2:T(2,128)S(1)}, u32[]{:S(2)}, u32[]{:S(2)}) collective-permute-start(f32[2,2,16,512]{3,1,0,2:T(2,128)S(1)} %broadcast_select_fusion.2), channel_id=1, source_target_pairs={{0,4},{1,5},{2,6},{3,7},{4,0},{5,1},{6,2},{7,3},{8,12},{9,13},{10,... | collective-permute-start | bytes 393224 | tf_op jit(solution)/shard_map/ppermute | solution.py:31
  166.2 6.0 %collective-permute-start.7 = (f32[2,2,8,512]{3,1,0,2:T(2,128)S(1)}, f32[2,2,8,512]{3,1,0,2:T(2,128)S(1)}, u32[]{:S(2)}, u32[]{:S(2)}) collective-permute-start(f32[2,2,8,512]{3,1,0,2:T(2,128)S(1)} %broadcast_select_fusion.3), channel_id=1, source_target_pairs={{0,2},{1,3},{2,0},{3,1},{4,6},{5,7},{6,4},{7,5},{8,10},{9,11},{10,... | collective-permute-start | bytes 196616 | tf_op jit(solution)/shard_map/ppermute | solution.py:31
  172.3 4.7 %collective-permute-start.9 = (f32[2,2,4,512]{3,1,0,2:T(2,128)S(1)}, f32[2,2,4,512]{3,1,0,2:T(2,128)S(1)}, u32[]{:S(2)}, u32[]{:S(2)}) collective-permute-start(f32[2,2,4,512]{3,1,0,2:T(2,128)S(1)} %broadcast_select_fusion.4), channel_id=1, source_target_pairs={{0,1},{1,0},{2,3},{3,2},{4,5},{5,4},{6,7},{7,6},{8,9},{9,8},{10,11... | collective-permute-start | bytes 98312 | tf_op jit(solution)/shard_map/ppermute | solution.py:31
where the time goes:
time: 181 us; the launch traced here: 178 us
  matrix products  53.1 us (29%)
  blocking collectives  53 us (29%)
  starting transfers between devices  30.1 us (17%)
  waiting for transfers between devices  20.3 us (11%)
  local copies, waits for them, and re-layouts  12.6 us (7%)
  other arithmetic  5.93 us (3%)
  between operations  1.9 us (1%)
    all_gather x1, blocking collectives, gather_together(): lines, at, gathered = (lax.all_gather(flat, axis), 0, [])  53 us
    ppermute x15, starting transfers between devices, partner(): return lax.ppermute(value, axis, pairs)  30.1 us
    dot_general x16, matrix products, step_forward(): jnp.dot(softmax_probs.astype(jnp.bfloat16), latent_block, preferred_eleme...  24.8 us
    dot_general x16, matrix products, step_forward(): jnp.einsum('qk,tk->qt', queries, latent_block, preferred_element_type=jnp...  22 us
    ppermute x15, waiting for transfers between devices, partner(): return lax.ppermute(value, axis, pairs)  20.3 us
    squeeze x1, local copies, waits for them, and re-layouts, on_device(): latent_cache[request]  5.88 us
    dot_general x16, matrix products, step_forward(): jnp.dot(rotary, rope_block, preferred_element_type=jnp.float32)  4.77 us
  transfers between devices with their start and end apart: 15, of which 9 were waited for; matrix products, arithmetic and copies ran while one was open for 3% of the time, Pallas kernels for 0%

commit v1 on v0

v1 whole, which is shorter than its diff:
```python
import functools

import jax
import jax.numpy as jnp
import numpy as np
from jax import lax
from jax.experimental import pallas as pl
from jax.experimental.pallas import tpu as pltpu
from jax.sharding import PartitionSpec as P

F32 = jnp.float32
BF16 = jnp.bfloat16
MASKED = -1e30
FLOOR = -1e29
NY, NZ = 4, 8
SHARDS = NY * NZ
REQS, STEPS, HEADS, NOPE, KVL, ROPE, VH = 2, 2, 4, 128, 512, 64, 128
ROWS = STEPS * HEADS
ALL = SHARDS * ROWS
KEYS = 4096
WIDE = KVL + 128
SCORE_SCALE = float((NOPE + ROPE) ** -0.5 * np.log2(np.e))
NT = (((1,), (1,)), ((), ()))
CHUNK1, SUB1 = 2048, 512
CHUNK2, SUB2 = 2048, 256
FAR_Z = (4, 3, 5, 2, 6, 1, 7)
FAR_Y = (2, 1, 3)


def iota(shape, dim):
    return lax.broadcasted_iota(jnp.int32, shape, dim)


def rounded(x):
    return x.astype(BF16).astype(F32)


def encode(maxima, totals):
    rows = maxima.shape[0]
    lane = iota((rows, 128), 1)
    high = rounded(maxima)
    middle = rounded(maxima - high)
    low = maxima - high - middle
    total_high = rounded(totals)
    total_low = totals - total_high
    tile = jnp.where(lane == 0, high, 0.0)
    tile = jnp.where(lane == 1, middle, tile)
    tile = jnp.where(lane == 2, low, tile)
    tile = jnp.where(lane == 3, total_high, tile)
    return jnp.where(lane == 4, total_low, tile)


def decode(tile):
    lane = iota(tile.shape, 1)
    maxima = jnp.sum(jnp.where(lane < 3, tile, 0.0), axis=1, keepdims=True)
    totals = jnp.sum(jnp.where(lane < 3, 0.0, tile), axis=1, keepdims=True)
    return maxima, totals


def merge(parts):
    highest = functools.reduce(jnp.maximum, [m for _, m, _ in parts])
    sums, totals = 0.0, 0.0
    for s, m, t in parts:
        factor = jnp.exp2(m - highest)
        sums = sums + s * factor
        totals = totals + t * factor
    return sums, highest, totals


def unpack(block):
    wide = block.astype(F32)
    return (wide[:, :KVL],) + decode(wide[:, KVL:])


def kernel(
    nope_ref, rope_ref, absorb_hbm, value_hbm, latent_hbm, keys_hbm,
    new_latent_ref, new_rope_ref, freq_ref, lengths_ref, positions_ref,
    out_ref,
    absorb, value, latent, keys, qa, qb, qfull, scores, acc, local_q,
    partial, yrecv, zsend, zrecv,
    load_sem, agz_s, agz_r, agy_s, agy_r, rsy_s, rsy_r, rsz_s, rsz_r,
):
    seq = lax.axis_index("seq")
    y = seq // NZ
    z = seq % NZ

    def at_z(d):
        return {"seq": y * NZ + (z + d) % NZ}

    def at_y(d):
        return {"seq": ((y + d) % NY) * NZ + z}

    barrier = pltpu.get_barrier_semaphore()
    for d in FAR_Z:
        pl.semaphore_signal(barrier, inc=1, device_id=at_z(d), device_id_type=pl.DeviceIdType.MESH)
    for d in FAR_Y:
        pl.semaphore_signal(barrier, inc=1, device_id=at_y(d), device_id_type=pl.DeviceIdType.MESH)

    loads = [
        pltpu.make_async_copy(absorb_hbm, absorb, load_sem.at[0]),
        pltpu.make_async_copy(latent_hbm.at[0], latent.at[0], load_sem.at[1]),
        pltpu.make_async_copy(keys_hbm, keys, load_sem.at[2]),
        pltpu.make_async_copy(latent_hbm.at[1], latent.at[1], load_sem.at[3]),
        pltpu.make_async_copy(value_hbm, value, load_sem.at[4]),
    ]
    for copy in loads:
        copy.start()

    rope_q = rope_ref[...].astype(F32)
    row8 = iota((ROWS, HEADS * ROPE), 0)
    lane256 = iota((ROWS, HEADS * ROPE), 1)
    fold_row = iota((HEADS * ROPE, 128), 0)
    fold_lane = iota((HEADS * ROPE, 128), 1)
    rope_tile = jnp.zeros((ROWS, 128), F32)
    for r in range(REQS):
        spread = jnp.where(row8 < HEADS, rope_q[r, 0:1], rope_q[r, 1:2])
        spread = jnp.where(lane256 // ROPE == row8 % HEADS, spread, 0.0).astype(BF16)
        fold = jnp.where(fold_row % ROPE + r * ROPE == fold_lane, 1.0, 0.0).astype(BF16)
        rope_tile = rope_tile + jnp.dot(spread, fold, preferred_element_type=F32)
    nope_q = nope_ref[...].astype(F32)
    row16 = iota((REQS * ROWS, NOPE), 0)
    spread = [jnp.where(row16 % HEADS == h, nope_q, 0.0) for h in range(HEADS)]
    spread = jnp.concatenate(spread, axis=1).astype(BF16)
    loads[0].wait()
    lat_q = jnp.dot(spread, absorb[...], preferred_element_type=F32).astype(BF16)
    local_q[...] = lat_q.astype(F32)
    lat_q = local_q[...]
    qa[seq, :, :KVL] = lat_q[:ROWS].astype(BF16)
    qa[seq, :, KVL:] = rope_tile.astype(BF16)
    qb[seq] = lat_q[ROWS:].astype(BF16)

    pl.semaphore_wait(barrier, NZ - 1 + NY - 1)

    queries = (qa, qb)

    def gather_z(r, d):
        mine = queries[r].at[seq]
        return pltpu.make_async_remote_copy(
            src_ref=mine, dst_ref=mine, send_sem=agz_s.at[r, d - 1], recv_sem=agz_r.at[r, d - 1],
            device_id=at_z(d), device_id_type=pl.DeviceIdType.MESH)

    def gather_y(r, d):
        mine = queries[r].at[pl.ds(y * NZ, NZ)]
        return pltpu.make_async_remote_copy(
            src_ref=mine, dst_ref=mine, send_sem=agy_s.at[r, d - 1], recv_sem=agy_r.at[r, d - 1],
            device_id=at_y(d), device_id_type=pl.DeviceIdType.MESH)

    def scatter_y(r, d):
        return pltpu.make_async_remote_copy(
            src_ref=partial.at[r, pl.ds(((y + d) % NY) * NZ, NZ)], dst_ref=yrecv.at[r, d - 1],
            send_sem=rsy_s.at[r, d - 1], recv_sem=rsy_r.at[r, d - 1],
            device_id=at_y(d), device_id_type=pl.DeviceIdType.MESH)

    def scatter_z(r, d):
        return pltpu.make_async_remote_copy(
            src_ref=zsend.at[r, (z + d) % NZ], dst_ref=zrecv.at[r, d - 1],
            send_sem=rsz_s.at[r, d - 1], recv_sem=rsz_r.at[r, d - 1],
            device_id=at_z(d), device_id_type=pl.DeviceIdType.MESH)

    for r in range(REQS):
        for d in FAR_Z:
            gather_z(r, d).start()

    freq = freq_ref[0:1]
    turn_sign = freq_ref[1:2]
    half_row = iota((ROPE, 128), 0)
    half_lane = iota((ROPE, 128), 1)
    new_latent = new_latent_ref[...].astype(F32)
    fresh = []
    lane_row = iota((8, 128), 0)
    positions = jnp.zeros((8, 128), jnp.int32)
    for r in range(REQS):
        for j in range(STEPS):
            positions = jnp.where(lane_row == r * STEPS + j, positions_ref[r, j], positions)
    angle = positions.astype(F32) * freq
    cosine, sine = jnp.cos(angle), jnp.sin(angle)
    row8n = iota((ROWS, 1), 0)
    for r in range(REQS):
        place = jnp.where(half_row + r * ROPE == half_lane, 1.0, 0.0).astype(BF16)
        swapped = jnp.where(
            (half_row + ROPE // 2) % ROPE + r * ROPE == half_lane, 1.0, 0.0).astype(BF16)
        plain = jnp.dot(new_rope_ref[...], place, preferred_element_type=F32)
        turned = jnp.dot(new_rope_ref[...], swapped, preferred_element_type=F32)
        found = []
        for j in range(STEPS):
            i = r * STEPS + j
            key = plain[i : i + 1] * cosine[i : i + 1] + turned[i : i + 1] * (sine[i : i + 1] * turn_sign)
            key = rounded(key)
            score = jnp.sum(lat_q[r * ROWS : (r + 1) * ROWS] * new_latent[r, j : j + 1], axis=1, keepdims=True)
            score = score + jnp.sum(rope_tile * key, axis=1, keepdims=True)
            found.append(jnp.where(row8n >= j * HEADS, score * SCORE_SCALE, MASKED))
        highest = functools.reduce(jnp.maximum, found)
        sums, totals = 0.0, 0.0
        for j in range(STEPS):
            weight = jnp.exp2(found[j] - highest)
            totals = totals + weight
            sums = sums + rounded(weight) * new_latent[r, j : j + 1]
        fresh.append((sums, highest, totals))

    for r in range(REQS):
        for d in FAR_Z:
            gather_z(r, d).wait_recv()
        for d in FAR_Y:
            gather_y(r, d).start()

    lane128 = iota((ALL, 128), 1)
    for r in range(REQS):
        for d in FAR_Y:
            gather_y(r, d).wait_recv()
        qfull[r] = queries[r][:, :, :KVL].astype(F32).reshape(ALL, KVL).astype(BF16)
        if r == 0:
            rotary = qa[:, :, KVL:].astype(F32).reshape(ALL, 128)
            loads[1].wait()
            loads[2].wait()
        else:
            loads[3].wait()
        own_rotary = jnp.where(lane128 // ROPE == r, rotary, 0.0).astype(BF16)
        query = qfull[r]
        live = lengths_ref[r] - seq * KEYS

        def score_chunk(c, peak):
            for i in range(CHUNK1 // SUB1):
                at = pl.multiple_of(c * CHUNK1 + i * SUB1, SUB1)
                s = lax.dot_general(query, latent[r, pl.ds(at, SUB1), :], NT, preferred_element_type=F32)
                s = s + jnp.dot(own_rotary, keys[:, pl.ds(at, SUB1)], preferred_element_type=F32)
                bias = jnp.where(at + iota((1, SUB1), 1) < live, 0.0, MASKED)
                s = s * SCORE_SCALE + bias
                scores[:, pl.ds(at, SUB1)] = s
                for t in range(SUB1 // 128):
                    peak = jnp.maximum(peak, s[:, t * 128 : (t + 1) * 128])
            return peak

        peak = lax.fori_loop(0, KEYS // CHUNK1, score_chunk, jnp.full((ALL, 128), FLOOR, F32))
        highest = jnp.max(peak, axis=1, keepdims=True)
        acc[...] = jnp.zeros_like(acc)

        def weigh_chunk(c, lane_sums):
            mixed = None
            for i in range(CHUNK2 // SUB2):
                at = pl.multiple_of(c * CHUNK2 + i * SUB2, SUB2)
                p = jnp.exp2(scores[:, pl.ds(at, SUB2)] - highest)
                for t in range(SUB2 // 128):
                    lane_sums = lane_sums + p[:, t * 128 : (t + 1) * 128]
                piece = jnp.dot(p.astype(BF16), latent[r, pl.ds(at, SUB2), :], preferred_element_type=F32)
                mixed = piece if mixed is None else mixed + piece
            acc[...] += mixed
            return lane_sums

        lane_sums = lax.fori_loop(0, KEYS // CHUNK2, weigh_chunk, jnp.zeros((ALL, 128), F32))
        totals = jnp.sum(lane_sums, axis=1, keepdims=True)
        partial[r, :, :, :KVL] = acc[...].reshape(SHARDS, ROWS, KVL).astype(BF16)
        partial[r, :, :, KVL:] = encode(highest, totals).reshape(SHARDS, ROWS, 128).astype(BF16)
        for d in FAR_Y:
            scatter_y(r, d).start()

    for r in range(REQS):
        parts = [unpack(partial[r, pl.ds(y * NZ, NZ)].astype(F32).reshape(NZ * ROWS, WIDE))]
        for d in (1, 3, 2):
            scatter_y(r, d).wait_recv()
            parts.append(unpack(yrecv[r, d - 1].astype(F32).reshape(NZ * ROWS, WIDE)))
        sums, highest, totals = merge(parts)
        zsend[r, :, :, :KVL] = sums.reshape(NZ, ROWS, KVL).astype(BF16)
        zsend[r, :, :, KVL:] = encode(highest, totals).reshape(NZ, ROWS, 128).astype(BF16)
        for d in FAR_Z:
            scatter_z(r, d).start()

    loads[4].wait()
    results = []
    for r in range(REQS):
        parts = [fresh[r], unpack(zsend[r, z].astype(F32))]
        for d in FAR_Z[::-1]:
            scatter_z(r, d).wait_recv()
            parts.append(unpack(zrecv[r, d - 1].astype(F32)))
        sums, highest, totals = merge(parts)
        results.append(rounded(sums / totals))
    result = jnp.concatenate(results, axis=0)
    row16v = iota((REQS * ROWS, KVL), 0)
    spread = [jnp.where(row16v % HEADS == h, result, 0.0) for h in range(HEADS)]
    spread = jnp.concatenate(spread, axis=1).astype(BF16)
    out_ref[...] = jnp.dot(spread, value[...], preferred_element_type=F32).astype(BF16)

    for r in range(REQS):
        for d in FAR_Z:
            gather_z(r, d).wait_send()
            scatter_z(r, d).wait_send()
        for d in FAR_Y:
            gather_y(r, d).wait_send()
            scatter_y(r, d).wait_send()


def frequency_rows():
    half = ROPE // 2
    lanes = np.arange(128)
    freq = (10000.0 ** (-(np.arange(half, dtype=np.float64)) / half)).astype(np.float32)
    sign = np.where(lanes % ROPE < half, -1.0, 1.0).astype(np.float32)
    return np.stack([freq[lanes % half], sign])


def on_device(
    query_nope, query_rope, key_absorb, value_up_matrix, latent_cache, rope_cache,
    new_latent, new_rope, lengths, positions,
):
    vmem = pl.BlockSpec(memory_space=pltpu.VMEM)
    smem = pl.BlockSpec(memory_space=pltpu.SMEM)
    hbm = pl.BlockSpec(memory_space=pl.ANY)
    out = pl.pallas_call(
        kernel,
        name="latent_attention",
        out_shape=jax.ShapeDtypeStruct((REQS * ROWS, VH), BF16),
        in_specs=[vmem, vmem, hbm, hbm, hbm, hbm, vmem, vmem, vmem, smem, smem],
        out_specs=vmem,
        scratch_shapes=[
            pltpu.VMEM((HEADS * NOPE, KVL), BF16),
            pltpu.VMEM((HEADS * KVL, VH), BF16),
            pltpu.VMEM((REQS, KEYS, KVL), BF16),
            pltpu.VMEM((REQS * ROPE, KEYS), BF16),
            pltpu.VMEM((SHARDS, ROWS, WIDE), BF16),
            pltpu.VMEM((SHARDS, ROWS, KVL), BF16),
            pltpu.VMEM((REQS, ALL, KVL), BF16),
            pltpu.VMEM((ALL, KEYS), F32),
            pltpu.VMEM((ALL, KVL), F32),
            pltpu.VMEM((REQS * ROWS, KVL), F32),
            pltpu.VMEM((REQS, SHARDS, ROWS, WIDE), BF16),
            pltpu.VMEM((REQS, NY - 1, NZ, ROWS, WIDE), BF16),
            pltpu.VMEM((REQS, NZ, ROWS, WIDE), BF16),
            pltpu.VMEM((REQS, NZ - 1, ROWS, WIDE), BF16),
            pltpu.SemaphoreType.DMA((5,)),
            pltpu.SemaphoreType.DMA((REQS, NZ - 1)),
            pltpu.SemaphoreType.DMA((REQS, NZ - 1)),
            pltpu.SemaphoreType.DMA((REQS, NY - 1)),
            pltpu.SemaphoreType.DMA((REQS, NY - 1)),
            pltpu.SemaphoreType.DMA((REQS, NY - 1)),
            pltpu.SemaphoreType.DMA((REQS, NY - 1)),
            pltpu.SemaphoreType.DMA((REQS, NZ - 1)),
            pltpu.SemaphoreType.DMA((REQS, NZ - 1)),
        ],
        compiler_params=pltpu.CompilerParams(collective_id=0, has_side_effects=True),
    )(
        query_nope.reshape(REQS * ROWS, NOPE),
        query_rope,
        key_absorb.reshape(HEADS * NOPE, KVL),
        value_up_matrix.reshape(HEADS * KVL, VH),
        latent_cache,
        rope_cache.reshape(REQS * ROPE, KEYS),
        new_latent,
        new_rope.reshape(REQS * STEPS, ROPE),
        jnp.asarray(frequency_rows()),
        lengths,
        positions,
    )
    return out.reshape(REQS, STEPS, HEADS, VH)


def solution(mesh):
    return jax.shard_map(
        on_device,
        mesh=mesh,
        in_specs=(
            P("req", None, "seq", None),
            P("req", None, "seq"),
            P("seq", None, None),
            P("seq", None, None),
            P("req", "seq", None),
            P("req", None, "seq"),
            P("req", None, None),
            P("req", None, None),
            P("req"),
            P("req", None),
        ),
        out_specs=P("req", None, "seq", None),
        check_vma=False,
    )
```

time: 181 us -> 39.7 us (0.22); the launches traced: 178 us -> 39.6 us
  matrix products: 53.1 us -> 0 us
  blocking collectives: 53 us -> 0 us
  Pallas kernels: 0 us -> 38.3 us
  starting transfers between devices: 30.1 us -> 0 us
  waiting for transfers between devices: 20.3 us -> 0 us
  local copies, waits for them, and re-layouts: 12.6 us -> 1.28 us
  other arithmetic: 5.93 us -> 0 us
  between operations: 1.9 us -> 0.01 us
    dot_general x52 -> x0, matrix products: 53.1 us -> none  [the longest x16 24.8 us: step_forward(): jnp.dot(softmax_probs.astype(jnp.bfloat16), latent_block, preferred_eleme...]
    all_gather x1 -> x0, blocking collectives: 53 us -> none  [gather_together(): lines, at, gathered = (lax.all_gather(flat, axis), 0, [])]
    pallas_call x0 -> x1, Pallas kernels: none -> 38.3 us  [on_device(): pl.pallas_call(kernel, name='latent_attention', out_shape=jax.ShapeDtypeS...]
    ppermute x15 -> x0, starting transfers between devices: 30.1 us -> none  [partner(): return lax.ppermute(value, axis, pairs)]
    ppermute x15 -> x0, waiting for transfers between devices: 20.3 us -> none  [partner(): return lax.ppermute(value, axis, pairs)]
    squeeze x2 -> x0, local copies, waits for them, and re-layouts: 5.95 us -> none  [the longest x1 5.88 us: on_device(): latent_cache[request]]
    reduce_sum x17 -> x0, other arithmetic: 2.56 us -> none  [the longest x16 2.48 us: step_forward(): return (weighted, highest, totals * shrink + jnp.sum(softmax_probs, axis=1))]
  transfers between devices with their start and end apart: 15 -> 0, of which waited for: 9 -> 0; matrix products, arithmetic and copies ran while one was open for 3% -> 0% of each run, Pallas kernels for 0% -> 0%
where the time goes in v1:
time: 39.7 us; the launch traced here: 39.6 us
  Pallas kernels  38.3 us (96%)
  local copies, waits for them, and re-layouts  1.28 us (3%)
    pallas_call x1, Pallas kernels, on_device(): pl.pallas_call(kernel, name='latent_attention', out_shape=jax.ShapeDtypeS...  38.3 us
    unnamed x1, local copies, waits for them, and re-layouts  1.28 us

profile of v1, /device:TPU:6, one launch (start us, length us, event | category | flops | bytes accessed | tf_op | source)
XLA Modules:
  0.0 39.6 jit_solution(7190217025148642627)
XLA Ops:
  0.0 38.3 %latent_attention.1 = bf16[16,128]{1,0:T(8,128)(2,1)} custom-call(bf16[16,128]{1,0:T(8,128)(2,1)} %bitcast.10, bf16[2,2,256]{2,1,0:T(2,128)(2,1)} %rope_ref.1, bf16[512,512]{1,0:T(8,128)(2,1)} %bitcast.7, bf16[2048,128]{1,0:T(8,128)(2,1)} %bitcast.8, bf16[2,4096,512]{2,1,0:T(8,128)(2,1)} %latent_hbm.1, bf16[128,4096]{1,0:T(8,128)(2,1)} %bitcast.6, ...), custom_call_target="tpu_custom_call" | custom-call | tf_op jit(solution)/shard_map/latent_attention/pallas_call | solution.py:306
  38.3 1.3 %copy.13 = bf16[2,2,4,128]{3,2,1,0:T(4,128)(2,1)} copy(bf16[2,2,4,128]{3,2,1,0:T(4,128)(2,1)} %bitcast.9) | data formatting | bytes 8192

commit v2 on v1

--- a/solution.py
+++ b/solution.py
@@ -20,11 +20,14 @@
 KEYS = 4096
 WIDE = KVL + 128
 SCORE_SCALE = float((NOPE + ROPE) ** -0.5 * np.log2(np.e))
-NT = (((1,), (1,)), ((), ()))
-CHUNK1, SUB1 = 2048, 512
-CHUNK2, SUB2 = 2048, 256
+SUB1 = 512
+SUB2 = 256
 FAR_Z = (4, 3, 5, 2, 6, 1, 7)
-FAR_Y = (2, 1, 3)
+NEAR_Z = (1, 7, 2, 6, 3, 5, 4)
+FAR_Y = (1, 3, 2)
+VMEM_LIMIT = 40 << 20
+GROUPS = (2, 1, 3, 0)
+GROUP = NZ * ROWS
 
 
 def iota(shape, dim):
@@ -72,13 +75,19 @@
     return (wide[:, :KVL],) + decode(wide[:, KVL:])
 
 
+def unpack_y(block, stats):
+    columns = stats.T
+    return block.astype(F32).reshape(GROUP, KVL), columns[:, 0:1], columns[:, 1:2]
+
+
 def kernel(
-    nope_ref, rope_ref, absorb_hbm, value_hbm, latent_hbm, keys_hbm,
-    new_latent_ref, new_rope_ref, freq_ref, lengths_ref, positions_ref,
+    nope_hbm, rope_hbm, absorb_hbm, value_hbm, latent_hbm, keys_hbm,
+    new_latent_hbm, new_rope_hbm, freq_hbm, lengths_hbm, positions_hbm,
     out_ref,
-    absorb, value, latent, keys, qa, qb, qfull, scores, acc, local_q,
-    partial, yrecv, zsend, zrecv,
-    load_sem, agz_s, agz_r, agy_s, agy_r, rsy_s, rsy_r, rsz_s, rsz_r,
+    nope_ref, rope_ref, new_latent_ref, new_rope_ref, freq_ref, lengths_ref, positions_ref,
+    absorb, value, latent, keys, qa, qb, qfull, rotary, flipped, scores, local_q,
+    partial, stats, yrecv, ystats, zsend, zrecv,
+    small_sem, load_sem, agz_s, agz_r, agy_s, agy_r, rsy_s, rsy_r, rst_s, rst_r, rsz_s, rsz_r,
 ):
     seq = lax.axis_index("seq")
     y = seq // NZ
@@ -96,6 +105,14 @@
     for d in FAR_Y:
         pl.semaphore_signal(barrier, inc=1, device_id=at_y(d), device_id_type=pl.DeviceIdType.MESH)
 
+    small = (
+        (nope_hbm, nope_ref), (rope_hbm, rope_ref), (new_latent_hbm, new_latent_ref),
+        (new_rope_hbm, new_rope_ref), (freq_hbm, freq_ref), (lengths_hbm, lengths_ref),
+        (positions_hbm, positions_ref),
+    )
+    small_loads = [pltpu.make_async_copy(a, b, small_sem.at[i]) for i, (a, b) in enumerate(small)]
+    for copy in small_loads:
+        copy.start()
     loads = [
         pltpu.make_async_copy(absorb_hbm, absorb, load_sem.at[0]),
         pltpu.make_async_copy(latent_hbm.at[0], latent.at[0], load_sem.at[1]),
@@ -106,6 +123,7 @@
     for copy in loads:
         copy.start()
 
+    small_loads[1].wait()
     rope_q = rope_ref[...].astype(F32)
     row8 = iota((ROWS, HEADS * ROPE), 0)
     lane256 = iota((ROWS, HEADS * ROPE), 1)
@@ -117,6 +135,7 @@
         spread = jnp.where(lane256 // ROPE == row8 % HEADS, spread, 0.0).astype(BF16)
         fold = jnp.where(fold_row % ROPE + r * ROPE == fold_lane, 1.0, 0.0).astype(BF16)
         rope_tile = rope_tile + jnp.dot(spread, fold, preferred_element_type=F32)
+    small_loads[0].wait()
     nope_q = nope_ref[...].astype(F32)
     row16 = iota((REQS * ROWS, NOPE), 0)
     spread = [jnp.where(row16 % HEADS == h, nope_q, 0.0) for h in range(HEADS)]
@@ -133,34 +152,59 @@
 
     queries = (qa, qb)
 
+    def settle(ref, sem):
+        pltpu.make_async_copy(ref, ref, sem).wait()
+
     def gather_z(r, d):
         mine = queries[r].at[seq]
         return pltpu.make_async_remote_copy(
-            src_ref=mine, dst_ref=mine, send_sem=agz_s.at[r, d - 1], recv_sem=agz_r.at[r, d - 1],
+            src_ref=mine, dst_ref=mine, send_sem=agz_s.at[r], recv_sem=agz_r.at[r, min(d, NZ - d) - 1],
             device_id=at_z(d), device_id_type=pl.DeviceIdType.MESH)
 
-    def gather_y(r, d):
-        mine = queries[r].at[pl.ds(y * NZ, NZ)]
+    def gather_y(r, d, k):
+        mine = queries[r].at[y * NZ + (z + k) % NZ]
         return pltpu.make_async_remote_copy(
-            src_ref=mine, dst_ref=mine, send_sem=agy_s.at[r, d - 1], recv_sem=agy_r.at[r, d - 1],
+            src_ref=mine, dst_ref=mine, send_sem=agy_s.at[r], recv_sem=agy_r.at[r, d - 1],
             device_id=at_y(d), device_id_type=pl.DeviceIdType.MESH)
+
+    def pass_on(r, distance):
+        senders = (distance,) if distance % (NZ // 2) == 0 else (distance, NZ - distance)
+        if distance:
+            settle(queries[r].at[pl.ds(0, len(senders))], agz_r.at[r, distance - 1])
+        for d in senders:
+            for e in FAR_Y:
+                gather_y(r, e, (NZ - d) % NZ).start()
+
+    def take_arrived(r, g):
+        settle(queries[r].at[pl.ds(0, NZ)], agy_r.at[r, NY - GROUPS[g] - 1])
+        take_group(r, g)
 
     def scatter_y(r, d):
         return pltpu.make_async_remote_copy(
-            src_ref=partial.at[r, pl.ds(((y + d) % NY) * NZ, NZ)], dst_ref=yrecv.at[r, d - 1],
-            send_sem=rsy_s.at[r, d - 1], recv_sem=rsy_r.at[r, d - 1],
+            src_ref=partial.at[r, GROUPS.index(d)], dst_ref=yrecv.at[r, d - 1],
+            send_sem=rsy_s.at[r], recv_sem=rsy_r.at[r],
+            device_id=at_y(d), device_id_type=pl.DeviceIdType.MESH)
+
+    def scatter_stats(r, d):
+        return pltpu.make_async_remote_copy(
+            src_ref=stats.at[r, GROUPS.index(d)], dst_ref=ystats.at[r, d - 1],
+            send_sem=rst_s.at[r], recv_sem=rst_r.at[r],
             device_id=at_y(d), device_id_type=pl.DeviceIdType.MESH)
 
     def scatter_z(r, d):
         return pltpu.make_async_remote_copy(
             src_ref=zsend.at[r, (z + d) % NZ], dst_ref=zrecv.at[r, d - 1],
-            send_sem=rsz_s.at[r, d - 1], recv_sem=rsz_r.at[r, d - 1],
+            send_sem=rsz_s.at[r], recv_sem=rsz_r.at[r],
             device_id=at_z(d), device_id_type=pl.DeviceIdType.MESH)
 
     for r in range(REQS):
-        for d in FAR_Z:
+        for d in NEAR_Z:
             gather_z(r, d).start()
 
+    pass_on(0, 0)
+
+    for copy in small_loads[2:]:
+        copy.wait()
     freq = freq_ref[0:1]
     turn_sign = freq_ref[1:2]
     half_row = iota((ROPE, 128), 0)
@@ -197,67 +241,88 @@
             sums = sums + rounded(weight) * new_latent[r, j : j + 1]
         fresh.append((sums, highest, totals))
 
-    for r in range(REQS):
-        for d in FAR_Z:
-            gather_z(r, d).wait_recv()
-        for d in FAR_Y:
-            gather_y(r, d).start()
-
-    lane128 = iota((ALL, 128), 1)
-    for r in range(REQS):
-        for d in FAR_Y:
-            gather_y(r, d).wait_recv()
-        qfull[r] = queries[r][:, :, :KVL].astype(F32).reshape(ALL, KVL).astype(BF16)
-        if r == 0:
-            rotary = qa[:, :, KVL:].astype(F32).reshape(ALL, 128)
-            loads[1].wait()
-            loads[2].wait()
-        else:
-            loads[3].wait()
-        own_rotary = jnp.where(lane128 // ROPE == r, rotary, 0.0).astype(BF16)
-        query = qfull[r]
+    lane128 = iota((GROUP, 128), 1)
+
+    def take_group(r, g):
+        rows = pl.ds(((y + GROUPS[g]) % NY) * NZ, NZ)
+        at = pl.ds(g * GROUP, GROUP)
+        qfull[r, at, :] = queries[r][rows, :, :KVL].astype(F32).reshape(GROUP, KVL).astype(BF16)
+        turned = qa[rows, :, KVL:].astype(F32).reshape(GROUP, 128)
+        rotary[r, at, :] = jnp.where(lane128 // ROPE == r, turned, 0.0).astype(BF16)
+
+    def score(r, first, count):
+        rows = pl.ds(first * GROUP, count * GROUP)
+        query, turned = qfull[r, rows, :], rotary[r, rows, :]
         live = lengths_ref[r] - seq * KEYS
-
-        def score_chunk(c, peak):
-            for i in range(CHUNK1 // SUB1):
-                at = pl.multiple_of(c * CHUNK1 + i * SUB1, SUB1)
-                s = lax.dot_general(query, latent[r, pl.ds(at, SUB1), :], NT, preferred_element_type=F32)
-                s = s + jnp.dot(own_rotary, keys[:, pl.ds(at, SUB1)], preferred_element_type=F32)
-                bias = jnp.where(at + iota((1, SUB1), 1) < live, 0.0, MASKED)
-                s = s * SCORE_SCALE + bias
-                scores[:, pl.ds(at, SUB1)] = s
-                for t in range(SUB1 // 128):
-                    peak = jnp.maximum(peak, s[:, t * 128 : (t + 1) * 128])
-            return peak
-
-        peak = lax.fori_loop(0, KEYS // CHUNK1, score_chunk, jnp.full((ALL, 128), FLOOR, F32))
-        highest = jnp.max(peak, axis=1, keepdims=True)
-        acc[...] = jnp.zeros_like(acc)
-
-        def weigh_chunk(c, lane_sums):
-            mixed = None
-            for i in range(CHUNK2 // SUB2):
-                at = pl.multiple_of(c * CHUNK2 + i * SUB2, SUB2)
-                p = jnp.exp2(scores[:, pl.ds(at, SUB2)] - highest)
-                for t in range(SUB2 // 128):
-                    lane_sums = lane_sums + p[:, t * 128 : (t + 1) * 128]
-                piece = jnp.dot(p.astype(BF16), latent[r, pl.ds(at, SUB2), :], preferred_element_type=F32)
-                mixed = piece if mixed is None else mixed + piece
-            acc[...] += mixed
-            return lane_sums
-
-        lane_sums = lax.fori_loop(0, KEYS // CHUNK2, weigh_chunk, jnp.zeros((ALL, 128), F32))
+        peak = jnp.full((count * GROUP, 128), FLOOR, F32)
+        for at in range(0, KEYS, SUB1):
+            s = jnp.dot(query, flipped[r, :, at : at + SUB1], preferred_element_type=F32)
+            s = s + jnp.dot(turned, keys[:, at : at + SUB1], preferred_element_type=F32)
+            bias = jnp.where(at + iota((1, SUB1), 1) < live, 0.0, MASKED)
+            s = s * SCORE_SCALE + bias
+            scores[rows, at : at + SUB1] = s
+            for t in range(SUB1 // 128):
+                peak = jnp.maximum(peak, s[:, t * 128 : (t + 1) * 128])
+        return jnp.max(peak, axis=1, keepdims=True)
+
+    def weigh(r, first, count, highest):
+        rows = pl.ds(first * GROUP, count * GROUP)
+        lane_sums = jnp.zeros((count * GROUP, 128), F32)
+        mixed = None
+        for at in range(0, KEYS, SUB2):
+            p = jnp.exp2(scores[rows, at : at + SUB2] - highest)
+            for t in range(SUB2 // 128):
+                lane_sums = lane_sums + p[:, t * 128 : (t + 1) * 128]
+            piece = jnp.dot(p.astype(BF16), latent[r, at : at + SUB2, :], preferred_element_type=F32)
+            mixed = piece if mixed is None else mixed + piece
         totals = jnp.sum(lane_sums, axis=1, keepdims=True)
-        partial[r, :, :, :KVL] = acc[...].reshape(SHARDS, ROWS, KVL).astype(BF16)
-        partial[r, :, :, KVL:] = encode(highest, totals).reshape(SHARDS, ROWS, 128).astype(BF16)
-        for d in FAR_Y:
-            scatter_y(r, d).start()
-
-    for r in range(REQS):
-        parts = [unpack(partial[r, pl.ds(y * NZ, NZ)].astype(F32).reshape(NZ * ROWS, WIDE))]
+        partial[r, pl.ds(first, count)] = mixed.reshape(count, NZ, ROWS, KVL).astype(BF16)
+        for g in range(first, first + count):
+            at = (g - first) * GROUP
+            pair = jnp.where(lane128 == 0, highest[at : at + GROUP], totals[at : at + GROUP])
+            stats[r, g] = pair.T[:8]
+            if GROUPS[g]:
+                scatter_y(r, GROUPS[g]).start()
+                scatter_stats(r, GROUPS[g]).start()
+
+    def flip(r, half):
+        for at in range(half * KEYS // 2, (half + 1) * KEYS // 2, SUB1):
+            flipped[r, :, at : at + SUB1] = latent[r, at : at + SUB1, :].T
+
+    loads[1].wait()
+    flip(0, 0)
+    pass_on(0, 1)
+    flip(0, 1)
+    pass_on(0, 2)
+    loads[2].wait()
+    loads[3].wait()
+    flip(1, 0)
+    pass_on(0, 3)
+    flip(1, 1)
+    pass_on(0, 4)
+    for distance in (0, 1, 2):
+        pass_on(1, distance)
+    take_group(0, 3)
+    highest = score(0, 3, 1)
+    for distance in (3, 4):
+        pass_on(1, distance)
+    weigh(0, 3, 1, highest)
+    for g in (1, 2, 0):
+        take_arrived(0, g)
+    weigh(0, 0, 3, score(0, 0, 3))
+    take_group(1, 3)
+    for g in (1, 2, 0):
+        take_arrived(1, g)
+    highest = score(1, 0, 4)
+    weigh(1, 0, 2, highest[: 2 * GROUP])
+    weigh(1, 2, 2, highest[2 * GROUP :])
+
+    for r in range(REQS):
+        parts = [unpack_y(partial[r, GROUPS.index(0)], stats[r, GROUPS.index(0)])]
+        settle(yrecv.at[r], rsy_r.at[r])
+        settle(ystats.at[r], rst_r.at[r])
         for d in (1, 3, 2):
-            scatter_y(r, d).wait_recv()
-            parts.append(unpack(yrecv[r, d - 1].astype(F32).reshape(NZ * ROWS, WIDE)))
+            parts.append(unpack_y(yrecv[r, d - 1], ystats[r, d - 1]))
         sums, highest, totals = merge(parts)
         zsend[r, :, :, :KVL] = sums.reshape(NZ, ROWS, KVL).astype(BF16)
         zsend[r, :, :, KVL:] = encode(highest, totals).reshape(NZ, ROWS, 128).astype(BF16)
@@ -268,8 +333,8 @@
     results = []
     for r in range(REQS):
         parts = [fresh[r], unpack(zsend[r, z].astype(F32))]
+        settle(zrecv.at[r], rsz_r.at[r])
         for d in FAR_Z[::-1]:
-            scatter_z(r, d).wait_recv()
             parts.append(unpack(zrecv[r, d - 1].astype(F32)))
         sums, highest, totals = merge(parts)
         results.append(rounded(sums / totals))
@@ -280,12 +345,11 @@
     out_ref[...] = jnp.dot(spread, value[...], preferred_element_type=F32).astype(BF16)
 
     for r in range(REQS):
-        for d in FAR_Z:
-            gather_z(r, d).wait_send()
-            scatter_z(r, d).wait_send()
-        for d in FAR_Y:
-            gather_y(r, d).wait_send()
-            scatter_y(r, d).wait_send()
+        settle(queries[r].at[pl.ds(0, NZ - 1)], agz_s.at[r])
+        settle(queries[r].at[pl.ds(0, (NY - 1) * NZ)], agy_s.at[r])
+        settle(partial.at[r, pl.ds(0, NY - 1)], rsy_s.at[r])
+        settle(stats.at[r, pl.ds(0, NY - 1)], rst_s.at[r])
+        settle(zsend.at[r, pl.ds(0, NZ - 1)], rsz_s.at[r])
 
 
 def frequency_rows():
@@ -301,15 +365,22 @@
     new_latent, new_rope, lengths, positions,
 ):
     vmem = pl.BlockSpec(memory_space=pltpu.VMEM)
-    smem = pl.BlockSpec(memory_space=pltpu.SMEM)
-    hbm = pl.BlockSpec(memory_space=pl.ANY)
+    hbm = pl.BlockSpec(memory_space=pltpu.HBM)
+    pin = lambda x: pltpu.with_memory_space_constraint(x, pltpu.HBM)
     out = pl.pallas_call(
         kernel,
         name="latent_attention",
         out_shape=jax.ShapeDtypeStruct((REQS * ROWS, VH), BF16),
-        in_specs=[vmem, vmem, hbm, hbm, hbm, hbm, vmem, vmem, vmem, smem, smem],
+        in_specs=[hbm] * 11,
         out_specs=vmem,
         scratch_shapes=[
+            pltpu.VMEM((REQS * ROWS, NOPE), BF16),
+            pltpu.VMEM((REQS, STEPS, HEADS * ROPE), BF16),
+            pltpu.VMEM((REQS, STEPS, KVL), BF16),
+            pltpu.VMEM((REQS * STEPS, ROPE), BF16),
+            pltpu.VMEM((2, 128), F32),
+            pltpu.SMEM((REQS,), jnp.int32),
+            pltpu.SMEM((REQS, STEPS), jnp.int32),
             pltpu.VMEM((HEADS * NOPE, KVL), BF16),
             pltpu.VMEM((HEADS * KVL, VH), BF16),
             pltpu.VMEM((REQS, KEYS, KVL), BF16),
@@ -317,25 +388,31 @@
             pltpu.VMEM((SHARDS, ROWS, WIDE), BF16),
             pltpu.VMEM((SHARDS, ROWS, KVL), BF16),
             pltpu.VMEM((REQS, ALL, KVL), BF16),
+            pltpu.VMEM((REQS, ALL, 128), BF16),
+            pltpu.VMEM((REQS, KVL, KEYS), BF16),
             pltpu.VMEM((ALL, KEYS), F32),
-            pltpu.VMEM((ALL, KVL), F32),
             pltpu.VMEM((REQS * ROWS, KVL), F32),
-            pltpu.VMEM((REQS, SHARDS, ROWS, WIDE), BF16),
-            pltpu.VMEM((REQS, NY - 1, NZ, ROWS, WIDE), BF16),
+            pltpu.VMEM((REQS, NY, NZ, ROWS, KVL), BF16),
+            pltpu.VMEM((REQS, NY, 8, GROUP), F32),
+            pltpu.VMEM((REQS, NY - 1, NZ, ROWS, KVL), BF16),
+            pltpu.VMEM((REQS, NY - 1, 8, GROUP), F32),
             pltpu.VMEM((REQS, NZ, ROWS, WIDE), BF16),
             pltpu.VMEM((REQS, NZ - 1, ROWS, WIDE), BF16),
+            pltpu.SemaphoreType.DMA((7,)),
             pltpu.SemaphoreType.DMA((5,)),
-            pltpu.SemaphoreType.DMA((REQS, NZ - 1)),
-            pltpu.SemaphoreType.DMA((REQS, NZ - 1)),
+            pltpu.SemaphoreType.DMA((REQS,)),
+            pltpu.SemaphoreType.DMA((REQS, NZ // 2)),
+            pltpu.SemaphoreType.DMA((REQS,)),
             pltpu.SemaphoreType.DMA((REQS, NY - 1)),
-            pltpu.SemaphoreType.DMA((REQS, NY - 1)),
-            pltpu.SemaphoreType.DMA((REQS, NY - 1)),
-            pltpu.SemaphoreType.DMA((REQS, NY - 1)),
-            pltpu.SemaphoreType.DMA((REQS, NZ - 1)),
-            pltpu.SemaphoreType.DMA((REQS, NZ - 1)),
+            pltpu.SemaphoreType.DMA((REQS,)),
+            pltpu.SemaphoreType.DMA((REQS,)),
+            pltpu.SemaphoreType.DMA((REQS,)),
+            pltpu.SemaphoreType.DMA((REQS,)),
+            pltpu.SemaphoreType.DMA((REQS,)),
+            pltpu.SemaphoreType.DMA((REQS,)),
         ],
-        compiler_params=pltpu.CompilerParams(collective_id=0, has_side_effects=True),
-    )(
+        compiler_params=pltpu.CompilerParams(collective_id=0, has_side_effects=True, vmem_limit_bytes=VMEM_LIMIT),
+    )(*map(pin, (
         query_nope.reshape(REQS * ROWS, NOPE),
         query_rope,
         key_absorb.reshape(HEADS * NOPE, KVL),
@@ -347,7 +424,7 @@
         jnp.asarray(frequency_rows()),
         lengths,
         positions,
-    )
+    )))
     return out.reshape(REQS, STEPS, HEADS, VH)
 
 

time: 39.7 us -> 34.4 us (0.87)
  Pallas kernels: 38.3 us -> 33.7 us
  local copies, waits for them, and re-layouts: 1.28 us -> 0.6 us
    pallas_call x1, Pallas kernels: 38.3 us -> 33.7 us  [on_device(): pl.pallas_call(kernel, name='latent_attention', out_shape=jax.ShapeDtypeS...]
    unnamed x1, local copies, waits for them, and re-layouts: 1.28 us -> 0.6 us
where the time goes in v2:
time: 34.4 us; the launch traced here: 34.3 us
  Pallas kernels  33.7 us (98%)
  local copies, waits for them, and re-layouts  0.6 us (2%)
    pallas_call x1, Pallas kernels, on_device(): pl.pallas_call(kernel, name='latent_attention', out_shape=jax.ShapeDtypeS...  33.7 us

profile of v2, /device:TPU:6, one launch (start us, length us, event | category | flops | bytes accessed | tf_op | source)
XLA Modules:
  0.0 34.3 jit_solution(8032729452296026172)
XLA Ops:
  0.0 33.7 %latent_attention.1 = bf16[16,128]{1,0:T(8,128)(2,1)S(1)} custom-call(bf16[16,128]{1,0:T(8,128)(2,1)} %bitcast.10, bf16[2,2,256]{2,1,0:T(2,128)(2,1)} %rope_hbm.1, bf16[512,512]{1,0:T(8,128)(2,1)} %bitcast.8, bf16[2048,128]{1,0:T(8,128)(2,1)} %bitcast.9, bf16[2,4096,512]{2,1,0:T(8,128)(2,1)} %latent_hbm.1, bf16[128,4096]{1,0:T(8,128)(2,1)} %bitcast.7, ...), custom_call_target="tpu_custom_call" | custom-call | tf_op jit(solution)/shard_map/latent_attention/pallas_call | solution.py:370
  33.7 0.6 %copy.13 = bf16[2,2,4,128]{3,2,1,0:T(4,128)(2,1)} copy(bf16[2,2,4,128]{3,2,1,0:T(4,128)(2,1)S(1)} %bitcast.6) | data formatting | bytes 8192

commit v3 on v2

--- a/solution.py
+++ b/solution.py
@@ -23,6 +23,9 @@
 SUB1 = 512
 SUB2 = 256
 FAR_Z = (4, 3, 5, 2, 6, 1, 7)
+ORDER_Z = FAR_Z + (0,)
+FAR = 3
+SPANS = (pl.ds(0, FAR), pl.ds(FAR, NZ - FAR))
 NEAR_Z = (1, 7, 2, 6, 3, 5, 4)
 FAR_Y = (1, 3, 2)
 VMEM_LIMIT = 40 << 20
@@ -75,18 +78,13 @@
     return (wide[:, :KVL],) + decode(wide[:, KVL:])
 
 
-def unpack_y(block, stats):
-    columns = stats.T
-    return block.astype(F32).reshape(GROUP, KVL), columns[:, 0:1], columns[:, 1:2]
-
-
 def kernel(
     nope_hbm, rope_hbm, absorb_hbm, value_hbm, latent_hbm, keys_hbm,
     new_latent_hbm, new_rope_hbm, freq_hbm, lengths_hbm, positions_hbm,
     out_ref,
     nope_ref, rope_ref, new_latent_ref, new_rope_ref, freq_ref, lengths_ref, positions_ref,
     absorb, value, latent, keys, qa, qb, qfull, rotary, flipped, scores, local_q,
-    partial, stats, yrecv, ystats, zsend, zrecv,
+    partial, stats, yfar, ynear, ystats, zsend, zrecv,
     small_sem, load_sem, agz_s, agz_r, agy_s, agy_r, rsy_s, rsy_r, rst_s, rst_r, rsz_s, rsz_r,
 ):
     seq = lax.axis_index("seq")
@@ -151,6 +149,7 @@
     pl.semaphore_wait(barrier, NZ - 1 + NY - 1)
 
     queries = (qa, qb)
+    yrecv = (yfar, ynear)
 
     def settle(ref, sem):
         pltpu.make_async_copy(ref, ref, sem).wait()
@@ -179,10 +178,10 @@
         settle(queries[r].at[pl.ds(0, NZ)], agy_r.at[r, NY - GROUPS[g] - 1])
         take_group(r, g)
 
-    def scatter_y(r, d):
+    def scatter_y(r, d, part):
         return pltpu.make_async_remote_copy(
-            src_ref=partial.at[r, GROUPS.index(d)], dst_ref=yrecv.at[r, d - 1],
-            send_sem=rsy_s.at[r], recv_sem=rsy_r.at[r],
+            src_ref=partial.at[r, GROUPS.index(d), SPANS[part]], dst_ref=yrecv[part].at[r, d - 1],
+            send_sem=rsy_s.at[r], recv_sem=rsy_r.at[r, part],
             device_id=at_y(d), device_id_type=pl.DeviceIdType.MESH)
 
     def scatter_stats(r, d):
@@ -193,13 +192,12 @@
 
     def scatter_z(r, d):
         return pltpu.make_async_remote_copy(
-            src_ref=zsend.at[r, (z + d) % NZ], dst_ref=zrecv.at[r, d - 1],
+            src_ref=zsend.at[r, ORDER_Z.index(d)], dst_ref=zrecv.at[r, d - 1],
             send_sem=rsz_s.at[r], recv_sem=rsz_r.at[r],
             device_id=at_z(d), device_id_type=pl.DeviceIdType.MESH)
 
-    for r in range(REQS):
-        for d in NEAR_Z:
-            gather_z(r, d).start()
+    for d in NEAR_Z:
+        gather_z(0, d).start()
 
     pass_on(0, 0)
 
@@ -244,10 +242,12 @@
     lane128 = iota((GROUP, 128), 1)
 
     def take_group(r, g):
-        rows = pl.ds(((y + GROUPS[g]) % NY) * NZ, NZ)
+        line = ((y + GROUPS[g]) % NY) * NZ
         at = pl.ds(g * GROUP, GROUP)
-        qfull[r, at, :] = queries[r][rows, :, :KVL].astype(F32).reshape(GROUP, KVL).astype(BF16)
-        turned = qa[rows, :, KVL:].astype(F32).reshape(GROUP, 128)
+        blocks = [line + (z + d) % NZ for d in ORDER_Z]
+        rows = [queries[r][i, :, :KVL].astype(F32) for i in blocks]
+        qfull[r, at, :] = jnp.concatenate(rows, axis=0).astype(BF16)
+        turned = jnp.concatenate([qa[i, :, KVL:].astype(F32) for i in blocks], axis=0)
         rotary[r, at, :] = jnp.where(lane128 // ROPE == r, turned, 0.0).astype(BF16)
 
     def score(r, first, count):
@@ -260,7 +260,7 @@
             s = s + jnp.dot(turned, keys[:, at : at + SUB1], preferred_element_type=F32)
             bias = jnp.where(at + iota((1, SUB1), 1) < live, 0.0, MASKED)
             s = s * SCORE_SCALE + bias
-            scores[rows, at : at + SUB1] = s
+            scores[r, rows, at : at + SUB1] = s
             for t in range(SUB1 // 128):
                 peak = jnp.maximum(peak, s[:, t * 128 : (t + 1) * 128])
         return jnp.max(peak, axis=1, keepdims=True)
@@ -270,7 +270,7 @@
         lane_sums = jnp.zeros((count * GROUP, 128), F32)
         mixed = None
         for at in range(0, KEYS, SUB2):
-            p = jnp.exp2(scores[rows, at : at + SUB2] - highest)
+            p = jnp.exp2(scores[r, rows, at : at + SUB2] - highest)
             for t in range(SUB2 // 128):
                 lane_sums = lane_sums + p[:, t * 128 : (t + 1) * 128]
             piece = jnp.dot(p.astype(BF16), latent[r, at : at + SUB2, :], preferred_element_type=F32)
@@ -281,9 +281,12 @@
             at = (g - first) * GROUP
             pair = jnp.where(lane128 == 0, highest[at : at + GROUP], totals[at : at + GROUP])
             stats[r, g] = pair.T[:8]
-            if GROUPS[g]:
-                scatter_y(r, GROUPS[g]).start()
-                scatter_stats(r, GROUPS[g]).start()
+        away = [d for d in GROUPS[first : first + count] if d]
+        for d in away:
+            scatter_stats(r, d).start()
+        for part in range(2):
+            for d in away:
+                scatter_y(r, d, part).start()
 
     def flip(r, half):
         for at in range(half * KEYS // 2, (half + 1) * KEYS // 2, SUB1):
@@ -292,6 +295,8 @@
     loads[1].wait()
     flip(0, 0)
     pass_on(0, 1)
+    for d in NEAR_Z:
+        gather_z(1, d).start()
     flip(0, 1)
     pass_on(0, 2)
     loads[2].wait()
@@ -300,39 +305,47 @@
     pass_on(0, 3)
     flip(1, 1)
     pass_on(0, 4)
+    take_group(0, 3)
+    own = [score(0, 3, 1)]
     for distance in (0, 1, 2):
         pass_on(1, distance)
-    take_group(0, 3)
-    highest = score(0, 3, 1)
     for distance in (3, 4):
         pass_on(1, distance)
-    weigh(0, 3, 1, highest)
-    for g in (1, 2, 0):
-        take_arrived(0, g)
-    weigh(0, 0, 3, score(0, 0, 3))
     take_group(1, 3)
-    for g in (1, 2, 0):
-        take_arrived(1, g)
-    highest = score(1, 0, 4)
-    weigh(1, 0, 2, highest[: 2 * GROUP])
-    weigh(1, 2, 2, highest[2 * GROUP :])
-
-    for r in range(REQS):
-        parts = [unpack_y(partial[r, GROUPS.index(0)], stats[r, GROUPS.index(0)])]
-        settle(yrecv.at[r], rsy_r.at[r])
-        settle(ystats.at[r], rst_r.at[r])
-        for d in (1, 3, 2):
-            parts.append(unpack_y(yrecv[r, d - 1], ystats[r, d - 1]))
-        sums, highest, totals = merge(parts)
-        zsend[r, :, :, :KVL] = sums.reshape(NZ, ROWS, KVL).astype(BF16)
-        zsend[r, :, :, KVL:] = encode(highest, totals).reshape(NZ, ROWS, 128).astype(BF16)
-        for d in FAR_Z:
-            scatter_z(r, d).start()
+    own.append(score(1, 3, 1))
+    for r in range(REQS):
+        for g in (1, 2, 0):
+            take_arrived(r, g)
+        highest = score(r, 0, 3)
+        weigh(r, 0, 2, highest[: 2 * GROUP])
+        weigh(r, 2, 2, jnp.concatenate([highest[2 * GROUP :], own[r]], axis=0))
+
+    for r in range(REQS):
+        for part in range(2):
+            first, count = (0, FAR) if part == 0 else (FAR, NZ - FAR)
+            settle(yrecv[part].at[r], rsy_r.at[r, part])
+            if part == 0:
+                settle(ystats.at[r], rst_r.at[r])
+                columns = [stats[r, GROUPS.index(0)].T] + [ystats[r, d - 1].T for d in (1, 3, 2)]
+            blocks = [partial[r, GROUPS.index(0), SPANS[part]]]
+            blocks = blocks + [yrecv[part][r, d - 1] for d in (1, 3, 2)]
+            parts = []
+            for block, column in zip(blocks, columns):
+                column = column[first * ROWS : (first + count) * ROWS]
+                block = block.astype(F32).reshape(count * ROWS, KVL)
+                parts.append((block, column[:, 0:1], column[:, 1:2]))
+            sums, highest, totals = merge(parts)
+            tile = encode(highest, totals)
+            zsend[r, SPANS[part], :, :KVL] = sums.reshape(count, ROWS, KVL).astype(BF16)
+            zsend[r, SPANS[part], :, KVL:] = tile.reshape(count, ROWS, 128).astype(BF16)
+            for d in ORDER_Z[first : first + count]:
+                if d:
+                    scatter_z(r, d).start()
 
     loads[4].wait()
     results = []
     for r in range(REQS):
-        parts = [fresh[r], unpack(zsend[r, z].astype(F32))]
+        parts = [fresh[r], unpack(zsend[r, ORDER_Z.index(0)].astype(F32))]
         settle(zrecv.at[r], rsz_r.at[r])
         for d in FAR_Z[::-1]:
             parts.append(unpack(zrecv[r, d - 1].astype(F32)))
@@ -390,11 +403,12 @@
             pltpu.VMEM((REQS, ALL, KVL), BF16),
             pltpu.VMEM((REQS, ALL, 128), BF16),
             pltpu.VMEM((REQS, KVL, KEYS), BF16),
-            pltpu.VMEM((ALL, KEYS), F32),
+            pltpu.VMEM((REQS, ALL, KEYS), F32),
             pltpu.VMEM((REQS * ROWS, KVL), F32),
             pltpu.VMEM((REQS, NY, NZ, ROWS, KVL), BF16),
             pltpu.VMEM((REQS, NY, 8, GROUP), F32),
-            pltpu.VMEM((REQS, NY - 1, NZ, ROWS, KVL), BF16),
+            pltpu.VMEM((REQS, NY - 1, FAR, ROWS, KVL), BF16),
+            pltpu.VMEM((REQS, NY - 1, NZ - FAR, ROWS, KVL), BF16),
             pltpu.VMEM((REQS, NY - 1, 8, GROUP), F32),
             pltpu.VMEM((REQS, NZ, ROWS, WIDE), BF16),
             pltpu.VMEM((REQS, NZ - 1, ROWS, WIDE), BF16),
@@ -405,7 +419,7 @@
             pltpu.SemaphoreType.DMA((REQS,)),
             pltpu.SemaphoreType.DMA((REQS, NY - 1)),
             pltpu.SemaphoreType.DMA((REQS,)),
-            pltpu.SemaphoreType.DMA((REQS,)),
+            pltpu.SemaphoreType.DMA((REQS, 2)),
             pltpu.SemaphoreType.DMA((REQS,)),
             pltpu.SemaphoreType.DMA((REQS,)),
             pltpu.SemaphoreType.DMA((REQS,)),

time: 34.4 us -> 33.3 us (0.968)
  Pallas kernels: 33.7 us -> 32.6 us
    pallas_call x1, Pallas kernels: 33.7 us -> 32.6 us  [on_device(): pl.pallas_call(kernel, name='latent_attention', out_shape=jax.ShapeDtypeS...]
where the time goes in v3:
time: 33.3 us; the launch traced here: 33.2 us
  Pallas kernels  32.6 us (98%)
  local copies, waits for them, and re-layouts  0.6 us (2%)
    pallas_call x1, Pallas kernels, on_device(): pl.pallas_call(kernel, name='latent_attention', out_shape=jax.ShapeDtypeS...  32.6 us

profile of v3, /device:TPU:6, one launch (start us, length us, event | category | flops | bytes accessed | tf_op | source)
XLA Modules:
  0.0 33.2 jit_solution(15075023746820237858)
XLA Ops:
  0.0 32.6 %latent_attention.1 = bf16[16,128]{1,0:T(8,128)(2,1)S(1)} custom-call(bf16[16,128]{1,0:T(8,128)(2,1)} %bitcast.10, bf16[2,2,256]{2,1,0:T(2,128)(2,1)} %rope_hbm.1, bf16[512,512]{1,0:T(8,128)(2,1)} %bitcast.8, bf16[2048,128]{1,0:T(8,128)(2,1)} %bitcast.9, bf16[2,4096,512]{2,1,0:T(8,128)(2,1)} %latent_hbm.1, bf16[128,4096]{1,0:T(8,128)(2,1)} %bitcast.7, ...), custom_call_target="tpu_custom_call" | custom-call | tf_op jit(solution)/shard_map/latent_attention/pallas_call | solution.py:383
  32.6 0.6 %copy.13 = bf16[2,2,4,128]{3,2,1,0:T(4,128)(2,1)} copy(bf16[2,2,4,128]{3,2,1,0:T(4,128)(2,1)S(1)} %bitcast.6) | data formatting | bytes 8192
